TPU v7x, 32 devices: a whole 2x2x4 slice. The times are simulated.
32 devices in a mesh: dom: 8 (over z, y), cls: 4 (over x, core).
Axes of the slice: x: 2, y: 2, z: 4, core: 2. Of those that a mesh axis runs over, the one named last changes fastest.
Arguments:
- images: bfloat16 [4096, 2, 16384], P(('dom', 'cls')), may hold values from -6 to 6
- slices: bfloat16 [32, 4, 2, 16384], P(('dom', 'cls')), may hold values from -6 to 6
- classes: int32 [4096], P(('dom', 'cls')), may hold values from 0 to 31, as said below
- rotations: int32 [4096], P(('dom', 'cls')), may hold values from 0 to 3
- defocus: int32 [4096], P(('dom', 'cls')), may hold values from 8000 to 29999
- groups: int32 [4096], P(('dom', 'cls')), may hold values from 0 to 255, as said below
Outputs:
- sigma: float32 [256, 64], P(('dom', 'cls'))
Inputs may be any that keep to these rules, and one draw needn't show every extreme that they name: Class c is owned by device c // 1 of dom+cls. In the rows of one device, at most 8 particles have classes of one owner; in every draw one owner gets exactly 8 from the rows of every device. `groups`: group g is owned by device g // 8 of dom+cls. Every group holds at least 8 particles.
All inputs are finite; a program needn't handle non-finite values.
Results may differ from a plain program's by a relative error of at most 0.0003.
Values may be sent and summed in bfloat16 or wider, within the bound.
A program may use at most 192 MiB of HBM per device.

v0:
```python
import math

import jax
import jax.numpy as jnp
from jax import lax
from jax.sharding import PartitionSpec as P

GROUPS_DEV = 8


PIXEL_SIZE = 1.5
WAVELENGTH = 0.0197
SPHERICAL = 27000000.0
AMPLITUDE = 0.1


def frequency_grid(side_cells):
    offsets = jnp.arange(side_cells, dtype=jnp.int32)
    signed = jnp.where(offsets < side_cells // 2, offsets, offsets - side_cells)
    return (signed[:, None] * signed[:, None] + signed[None, :] * signed[None, :]).reshape(-1)


def shell_matrix(radius_sq, shell_count):
    shell_ids = jnp.arange(shell_count, dtype=jnp.int32)
    lower = shell_ids * shell_ids
    upper = (shell_ids + 1) * (shell_ids + 1)
    in_shell = (lower[None, :] <= radius_sq[:, None]) & (radius_sq[:, None] < upper[None, :])
    return in_shell.astype(jnp.float32)


def contrast(defocus, radius_sq, side_cells):
    spatial = radius_sq.astype(jnp.float32) / jnp.float32((side_cells * PIXEL_SIZE) ** 2)
    depth = defocus.astype(jnp.float32)[:, None]
    phase_shift = (
        math.pi * WAVELENGTH * depth * spatial[None, :]
        - 0.5 * math.pi * SPHERICAL * WAVELENGTH**3 * spatial[None, :] * spatial[None, :]
    )
    return -(
        math.sqrt(1.0 - AMPLITUDE * AMPLITUDE) * jnp.sin(phase_shift)
        + AMPLITUDE * jnp.cos(phase_shift)
    )


def power_in_shells(images, fetched, ctf, shell_table):
    difference = images.astype(jnp.float32) - ctf[:, None, :] * fetched.astype(jnp.float32)
    pixel_power = jnp.sum(difference * difference, axis=1)
    return jnp.dot(
        pixel_power,
        shell_table,
        precision=lax.Precision.HIGHEST,
        preferred_element_type=jnp.float32,
    )


def body(images, slices, classes, rotations, defocus, groups):
    device_count = lax.axis_size(("dom", "cls"))
    per_device = images.shape[0]
    pixel_count = images.shape[2]
    rotation_count = slices.shape[1]
    side_cells = math.isqrt(pixel_count)
    empty = jnp.zeros((per_device, 2, pixel_count), jnp.bfloat16)
    shard_rows = lax.all_gather(slices, ("dom", "cls"), axis=0, tiled=True)
    shard_count = shard_rows.shape[0]
    in_range = (classes >= 0) & (classes < shard_count)
    row_index = jnp.clip(classes, 0, shard_count - 1) * rotation_count + rotations
    picked = shard_rows.reshape(shard_count * rotation_count, 2, pixel_count)[row_index]
    fetched = jnp.where(in_range[:, None, None], picked, empty)
    radius_sq = frequency_grid(side_cells)
    shell_table = shell_matrix(radius_sq, side_cells // 2)
    ctf = contrast(defocus, radius_sq, side_cells)
    shell_power = power_in_shells(images, fetched, ctf, shell_table)
    group_total = GROUPS_DEV * device_count
    group_table = (groups[:, None] == jnp.arange(group_total, dtype=jnp.int32)[None, :]).astype(
        jnp.float32
    )
    partial_sums = lax.dot_general(
        group_table,
        shell_power,
        (((0,), (0,)), ((), ())),
        precision=lax.Precision.HIGHEST,
        preferred_element_type=jnp.float32,
    )
    partial_counts = jnp.sum(group_table, axis=0)
    group_sums, group_counts = (
        lax.psum_scatter(partial_sums, ("dom", "cls"), scatter_dimension=0, tiled=True),
        lax.psum_scatter(partial_counts, ("dom", "cls"), scatter_dimension=0, tiled=True),
    )
    pixel_counts = jnp.sum(shell_table, axis=0)
    return group_sums / (2.0 * group_counts[:, None] * pixel_counts[None, :])


def solution(mesh):
    return jax.shard_map(
        body,
        mesh=mesh,
        in_specs=(
            P(("dom", "cls"), None, None),
            P(("dom", "cls"), None, None, None),
            P(("dom", "cls")),
            P(("dom", "cls")),
            P(("dom", "cls")),
            P(("dom", "cls")),
        ),
        out_specs=P(("dom", "cls"), None),
        check_vma=False,
    )
```

profile of v0, /device:TPU:0, one launch (start us, length us, event | category | flops | bytes accessed | tf_op | source)
XLA Modules:
  0.0 307.1 jit_solution(8819084028001835942)
XLA Ops:
  6.5 0.0 all-gather.2.cloned.1.call-start
  6.5 1.8 copy.9
  8.4 0.0 all-gather.2.cloned.1.call-update
  8.4 0.0 all-reduce.4.cloned.1.call-start
  8.5 0.8 convert_reduce_fusion.1
  9.2 42.6 %all-reduce.1 = f32[256]{0:T(256)S(1)} all-reduce(f32[256]{0:T(256)S(1)} %convert_reduce_fusion.1), channel_id=3, replica_groups=mesh['dom'=8,'cls'=4] {'dom','cls'}, use_global_device_ids=true, to_apply=%region_3.4.clone | all-reduce | flops 256 | bytes 2048
  51.9 0.7 compare_select_fusion
  52.5 0.1 add_bitcast_fusion
  52.6 0.9 convert_reduce_fusion
  53.5 0.7 compare_and_fusion.2
  54.2 0.7 convert_multiply_fusion.1
  54.8 0.1 convert_multiply_fusion
  54.9 32.0 %add_negate_fusion = f32[128,16384]{1,0:T(8,128)} fusion(f32[16384]{0:T(1024)S(1)} %get-tuple-element.6, f32[16384]{0:T(1024)S(1)} %get-tuple-element.5, f32[128]{0:T(128)S(1)} %convert_multiply_fusion.1), kind=kLoop, calls=%fused_computation.3 | loop fusion | flops 12582912 | bytes 8520192 | tf_op jit(solution)/shard_map/neg | solution.py:38
  86.9 3.3 %all-gather.2.cloned.1.call-done = bf16[32,4,2,16384]{3,1,2,0:T(4,128)(2,1)} async-done(((bf16[1,4,2,16384]{3,1,2,0:T(4,128)(2,1)}), bf16[32,4,2,16384]{3,1,2,0:T(4,128)(2,1)}) %all-gather.2.cloned.1.call-update) | async-done | bytes 8388624 | tf_op jit(solution)/shard_map/all_gather | solution.py:62
  90.3 16.3 %copy.10 = bf16[32,4,2,16384]{3,2,1,0:T(2,128)(2,1)} copy(bf16[32,4,2,16384]{3,1,2,0:T(4,128)(2,1)} %all-gather.2.cloned.1.call-done) | data formatting | bytes 16777216 | tf_op jit(solution)/shard_map/all_gather | solution.py:62
  106.6 23.2 %gather_fusion = bf16[128,2,16384]{2,1,0:T(2,128)(2,1)} fusion(bf16[128,2,16384]{2,1,0:T(2,128)(2,1)} %bitcast.11, s32[1024]{0:T(1024)S(1)} %pad_clamp_fusion), kind=kCustom, calls=%fused_computation | custom fusion | bytes 16777728 | tf_op jit(solution)/shard_map/gather | solution.py:66
  129.7 37.1 %multiply_reduce_fusion = f32[128,16384]{1,0:T(8,128)} fusion(bf16[128,2,16384]{2,1,0:T(2,128)(2,1)} %param.6, bf16[128,2,16384]{2,1,0:T(2,128)(2,1)} %gather_fusion, pred[128]{0:T(512)(128)(4,1)S(1)} %compare_and_fusion.2, f32[128,16384]{1,0:T(8,128)} %add_negate_fusion), kind=kLoop, calls=%fused_computation.1 | loop fusion | flops 27262976 | bytes 33554560 | tf_op jit(solution)/shard_map/reduce_sum | solution.py:46
  166.9 7.7 %fusion = f32[128,64]{0,1:T(8,128)S(1)} fusion(f32[128,16384]{1,0:T(8,128)} %multiply_reduce_fusion, s32[16384]{0:T(1024)S(1)} %add_bitcast_fusion, s32[64]{0:T(128)S(1)} %get-tuple-element.7, s32[64]{0:T(128)S(1)} %get-tuple-element.8), kind=kOutput, calls=%fused_computation.6 | convolution fusion | flops 1613758464 | bytes 8487424 | tf_op jit(solution)/shard_map/dot_general | solution.py:47
  174.6 0.0 copy-done
  174.6 1.0 fusion.5
  175.6 0.0 all-reduce.4.cloned.1.call-update
  175.6 0.1 dynamic-slice_multiply_fusion
  175.7 123.2 %all-reduce.4.cloned.1.call-done = f32[256,64]{1,0:T(8,128)} async-done(((f32[256,64]{1,0:T(8,128)}), f32[256,64]{1,0:T(8,128)}) %all-reduce.4.cloned.1.call-update) | async-done | bytes 65552
  298.9 1.3 dynamic-slice_divide_fusion
  (4 shorter events, 0.0 us)
Async XLA Ops:
  6.5 83.8 %all-gather.2.cloned.1.call-start = ((), (), s32[]{:S(2)}) async-start(), calls=%async_computation | async-start | bytes 8650752 | tf_op jit(solution)/shard_map/all_gather | solution.py:62
  8.4 290.5 %all-reduce.4.cloned.1.call-start = ((), (), s32[]{:S(2)}) async-start(), calls=%async_computation.1 | async-start | bytes 262144
  166.9 7.7 %copy-start = (s32[128]{0:T(128)S(1)}, s32[128]{0:T(128)}, u32[]{:S(2)}) copy-start(s32[128]{0:T(128)} %param.11) | copy-start | bytes 1540
Sparse Core Ops, SparseCore 0:
  10.2 80.0 all-gather.1
  175.8 123.1 all-reduce.3
where the time goes:
time: 307 us
  waiting for transfers between devices  127 us (41%)
  other arithmetic  74.4 us (24%)
  blocking collectives  42.6 us (14%)
  local copies, waits for them, and re-layouts  41.3 us (13%)
  between operations  13.4 us (4%)
  matrix products  8.71 us (3%)
    unnamed x3, waiting for transfers between devices  123 us
    unnamed x1, blocking collectives  42.6 us
    reduce_sum x1, other arithmetic, power_in_shells(): pixel_power = jnp.sum(difference * difference, axis=1)  37.1 us
    neg x1, other arithmetic, contrast(): -(math.sqrt(1.0 - AMPLITUDE * AMPLITUDE) * jnp.sin(phase_shift) + AMPLITU...  32 us
    gather x1, local copies, waits for them, and re-layouts, body(): shard_rows.reshape(shard_count * rotation_count, 2, pixel_count)[row_index]  23.2 us
    all_gather x1, local copies, waits for them, and re-layouts, body(): shard_rows = lax.all_gather(slices, ('dom', 'cls'), axis=0, tiled=True)  16.3 us
    dot_general x1, matrix products, power_in_shells(): jnp.dot(pixel_power, shell_table, precision=lax.Precision.HIGHEST, prefer...  7.72 us
  transfers between devices with their start and end apart: 2, of which 2 were waited for; matrix products, arithmetic and copies ran while one was open for 12% of the time, Pallas kernels for 0%

commit v1 on v0

v1 whole, which is shorter than its diff:
```python
import functools
import math

import jax
import jax.numpy as jnp
import numpy as np
from jax import lax
from jax.experimental import pallas as pl
from jax.experimental.pallas import tpu as pltpu
from jax.sharding import PartitionSpec as P

GROUPS_DEV = 8
PIXEL_SIZE = 1.5
WAVELENGTH = 0.0197
SPHERICAL = 27000000.0
AMPLITUDE = 0.1
MESH = pl.DeviceIdType.MESH
AXES = ("dom", "cls")
ROUTES = (("x", "y", "z"), ("z", "y", "x"), ("z", "x", "y"))
SHARE = (8, 12, 12)


def sine_coefficients(terms):
    nodes = 0.5 * np.cos((np.arange(400) + 0.5) * math.pi / 400)
    nodes = nodes[np.abs(nodes) > 1e-3]
    basis = np.stack([nodes ** (2 * k + 1) for k in range(terms)], 1)
    return np.linalg.lstsq(basis, np.sin(2 * math.pi * nodes), rcond=None)[0]


SINE = [float(v) for v in sine_coefficients(6)]


def gather_kernel(shape, own_ref, out_ref, local_sem, send_sem, recv_sem, pair_send, pair_recv):
    size = dict(x=shape[0], y=shape[1], z=shape[2])
    dom, cls = lax.axis_index("dom"), lax.axis_index("cls")
    here = dict(x=cls // 2, y=dom % size["y"], z=dom // size["y"])
    core = cls % 2
    rows = out_ref.shape[2]
    starts = [0]
    for share in SHARE:
        starts.append(starts[-1] + rows * share // 32)

    def device(at, which):
        return (at["z"] * size["y"] + at["y"], at["x"] * 2 + which)

    def slot(at, which):
        d = device(at, which)
        return d[0] * (size["x"] * 2) + d[1]

    def moved(at, dim, step):
        new = dict(at)
        new[dim] = at[dim] + step
        return new

    ways = []
    for dim in "xyz":
        if size[dim] == 1:
            continue
        if size[dim] == 2:
            other = dict(here)
            other[dim] = 1 - here[dim]
            ways.append((dim, 0, other, None))
        else:
            ways.append((dim, 1, moved(here, dim, 1), here[dim] < size[dim] - 1))
            ways.append((dim, -1, moved(here, dim, -1), here[dim] > 0))

    def when(conds, fn):
        conds = [c for c in conds if c is not None]
        if not conds:
            fn()
        else:
            pl.when(functools.reduce(jnp.logical_and, conds))(fn)

    barrier = pltpu.get_barrier_semaphore()
    partner = device(here, 1 - core)
    pl.semaphore_signal(barrier, inc=1, device_id=partner, device_id_type=MESH)
    for dim, sign, other, ok in ways:

        def greet(other=other):
            pl.semaphore_signal(barrier, inc=1, device_id=device(other, core), device_id_type=MESH)

        when([ok], greet)
    peers = 1
    for dim, sign, other, ok in ways:
        peers = peers + (1 if ok is None else ok.astype(jnp.int32))
    pl.semaphore_wait(barrier, peers)

    mine = slot(here, core)
    local = pltpu.make_async_copy(own_ref, out_ref.at[mine], local_sem)
    local.start()

    def part(ref, index):
        return ref.at[:, pl.ds(starts[index], starts[index + 1] - starts[index]), :]

    def copy(index, source, src_slot, to, way, own):
        src = part(own_ref, index) if own else part(out_ref.at[src_slot], index)
        return pltpu.make_async_remote_copy(
            src_ref=src,
            dst_ref=part(out_ref.at[src_slot], index),
            send_sem=send_sem.at[index, source, way],
            recv_sem=recv_sem.at[index, src_slot],
            device_id=to,
            device_id_type=MESH,
        )

    def pair_copy(index, source, src_slot, own):
        src = part(own_ref, index) if own else part(out_ref.at[src_slot], index)
        return pltpu.make_async_remote_copy(
            src_ref=src,
            dst_ref=part(out_ref.at[src_slot], index),
            send_sem=pair_send.at[index, source],
            recv_sem=pair_recv.at[index, src_slot],
            device_id=partner,
            device_id_type=MESH,
        )

    choices = {}
    for dim in "xyz":
        n = size[dim]
        if n == 1:
            choices[dim] = [(0, here[dim], None, 0)]
        elif n == 2:
            choices[dim] = [(0, here[dim], None, 0), (0, 1 - here[dim], None, 1)]
        else:
            listed = [(0, here[dim], None, 0)]
            for t in range(1, n):
                listed.append((1, here[dim] - t, here[dim] >= t, t))
                listed.append((-1, here[dim] + t, here[dim] + t < n, t))
            choices[dim] = listed
    events = []
    for ix, cx in enumerate(choices["x"]):
        for iy, cy in enumerate(choices["y"]):
            for iz, cz in enumerate(choices["z"]):
                pick = dict(x=cx, y=cy, z=cz)
                depth = cx[3] + cy[3] + cz[3]
                number = (ix * len(choices["y"]) + iy) * len(choices["z"]) + iz
                for index in range(3):
                    events.append((depth, index, number, pick))
    events.sort(key=lambda e: e[:3])
    finish = []
    for depth, index, number, pick in events:
        at = {dim: pick[dim][1] for dim in "xyz"}
        exists = [pick[dim][2] for dim in "xyz"]
        src_slot = slot(at, core)
        order = ROUTES[index]
        last = max([k for k, dim in enumerate(order) if pick[dim][3] > 0], default=-1)
        sends = []
        for number_way, (dim, sign, other, ok) in enumerate(ways):
            k = order.index(dim)
            if k < last:
                continue
            if k == last and (size[dim] == 2 or sign != pick[dim][0]):
                continue
            sends.append((number_way, device(other, core), ok))

        def arrive(index=index, number=number, src_slot=src_slot, depth=depth, sends=sends):
            own = depth == 0
            if not own:
                copy(index, number, src_slot, partner, 0, False).wait_recv()
            for way, to, ok in sends:
                when([ok], copy(index, number, src_slot, to, way, own).start)
            pair_copy(index, number, src_slot, own).start()

        def done(index=index, number=number, src_slot=src_slot, depth=depth, sends=sends, at=at):
            own = depth == 0
            for way, to, ok in sends:
                when([ok], copy(index, number, src_slot, to, way, own).wait_send)
            pair_copy(index, number, src_slot, own).wait_send()
            pair_copy(index, number, slot(at, 1 - core), False).wait_recv()

        when(exists, arrive)
        finish.append((exists, done))
    for exists, done in finish:
        when(exists, done)
    local.wait()


def gather(shape, own):
    devices = 2 * shape[0] * shape[1] * shape[2]
    total = 1
    for n in shape:
        total *= n if n <= 2 else 2 * n - 1
    return pl.pallas_call(
        functools.partial(gather_kernel, shape),
        out_shape=jax.ShapeDtypeStruct((devices,) + own.shape, own.dtype),
        in_specs=[pl.BlockSpec(memory_space=pltpu.VMEM)],
        out_specs=pl.BlockSpec(memory_space=pltpu.VMEM),
        scratch_shapes=[
            pltpu.SemaphoreType.DMA,
            pltpu.SemaphoreType.DMA((3, total, 4)),
            pltpu.SemaphoreType.DMA((3, devices)),
            pltpu.SemaphoreType.DMA((3, total)),
            pltpu.SemaphoreType.DMA((3, devices)),
        ],
        compiler_params=pltpu.CompilerParams(
            collective_id=0, has_side_effects=True, vmem_limit_bytes=32 * 1024 * 1024
        ),
        name="gather_slices",
    )(own)


def power_kernel(
    side, rot_count, index_ref, depth_ref, images_ref, slices_ref, slope_ref, offset_ref, groups_ref, out_ref, power, acc
):
    step = pl.program_id(0)
    count, chunk, lanes = images_ref.shape
    shells = side // 2

    @pl.when(step == 0)
    def _():
        acc[...] = jnp.zeros_like(acc)

    slope = slope_ref[...]
    offset = offset_ref[...]

    def one(i, carry):
        turns = depth_ref[i] * slope + offset
        x = turns - jnp.round(turns)
        y = x * x
        s = jnp.full_like(y, SINE[-1])
        for value in SINE[-2::-1]:
            s = s * y + value
        s = s * x
        d = images_ref[i].astype(jnp.float32) + s * slices_ref[index_ref[i], pl.ds(pl.multiple_of(step * chunk, chunk), chunk), :].astype(jnp.float32)
        power[pl.ds(pl.multiple_of(i * chunk, chunk), chunk), :] = d * d
        return carry

    lax.fori_loop(0, count, one, 0, unroll=4)

    b = lax.broadcasted_iota(jnp.int32, (lanes, shells), 0)
    s = lax.broadcasted_iota(jnp.int32, (lanes, shells), 1)
    fb = jnp.where(b < side // 2, b, b - side)
    total = acc[...]
    for k in range(chunk // 2):
        a = step * (chunk // 2) + k
        fa = jnp.where(a < side // 2, a, a - side)
        r = fa * fa + fb * fb
        table = jnp.where((s * s <= r) & (r < (s + 1) * (s + 1)), 1.0, 0.0).astype(jnp.bfloat16)
        p = power[pl.ds(2 * k, count, stride=chunk), :] + power[pl.ds(2 * k + 1, count, stride=chunk), :]
        high = p.astype(jnp.bfloat16)
        low = (p - high.astype(jnp.float32)).astype(jnp.bfloat16)
        total = total + (
            jnp.dot(high, table, preferred_element_type=jnp.float32)
            + jnp.dot(low, table, preferred_element_type=jnp.float32)
        )
    acc[...] = total

    @pl.when(step == pl.num_programs(0) - 1)
    def _():
        groups = out_ref.shape[0]
        ids = lax.broadcasted_iota(jnp.int32, (groups, count), 0)
        member = jnp.where(ids == groups_ref[...], 1.0, 0.0)
        both = jnp.concatenate([acc[...], jnp.ones((count, out_ref.shape[1] - shells), jnp.float32)], axis=1)
        out_ref[...] = jnp.dot(
            member, both, precision=lax.Precision.HIGHEST, preferred_element_type=jnp.float32
        )


def shell_power(images, slices, index, defocus, groups, group_total):
    count, rows, side = images.shape
    chunk = 32
    offsets = np.arange(side)
    signed = np.where(offsets < side // 2, offsets, offsets - side)
    radius = (signed[:, None] ** 2 + signed[None, :] ** 2).astype(np.float64)
    spatial = np.repeat(radius / (side * PIXEL_SIZE) ** 2, 2, axis=0)
    slope = (0.5 * WAVELENGTH * spatial).astype(np.float32)
    offset = -0.25 * SPHERICAL * WAVELENGTH**3 * spatial**2 + math.asin(AMPLITUDE) / (2 * math.pi)
    offset = (offset - np.round(offset)).astype(np.float32)
    smem = pl.BlockSpec(memory_space=pltpu.SMEM)
    return pl.pallas_call(
        functools.partial(power_kernel, side, 4),
        grid=(rows // chunk,),
        out_shape=jax.ShapeDtypeStruct((group_total, 128), jnp.float32),
        in_specs=[
            smem,
            smem,
            pl.BlockSpec((count, chunk, side), lambda i: (0, i, 0)),
            pl.BlockSpec(memory_space=pltpu.VMEM),
            pl.BlockSpec((chunk, side), lambda i: (i, 0)),
            pl.BlockSpec((chunk, side), lambda i: (i, 0)),
            pl.BlockSpec((1, count), lambda i: (0, 0)),
        ],
        out_specs=pl.BlockSpec((group_total, 128), lambda i: (0, 0)),
        scratch_shapes=[
            pltpu.VMEM((count * chunk, side), jnp.float32),
            pltpu.VMEM((count, side // 2), jnp.float32),
        ],
        compiler_params=pltpu.CompilerParams(vmem_limit_bytes=48 * 1024 * 1024),
        name="shell_power",
    )(index, defocus.astype(jnp.float32), images, slices, jnp.asarray(slope), jnp.asarray(offset), groups.reshape(1, count))


def exchange_kernel(sizes, shells, parts_ref, weight_ref, out_ref, held, send_sem, recv_sem):
    doms, clss = sizes
    n = doms * clss
    me = lax.axis_index("dom") * clss + lax.axis_index("cls")
    barrier = pltpu.get_barrier_semaphore()

    def device(k):
        peer = lax.rem(me + k, n)
        return peer, (peer // clss, lax.rem(peer, clss))

    def greet(k, carry):
        pl.semaphore_signal(barrier, inc=1, device_id=device(k)[1], device_id_type=MESH)
        return carry

    lax.fori_loop(1, n, greet, 0)
    pl.semaphore_wait(barrier, n - 1)

    def copy(k):
        peer, to = device(k)
        return pltpu.make_async_remote_copy(
            src_ref=parts_ref.at[peer],
            dst_ref=held.at[k],
            send_sem=send_sem.at[k],
            recv_sem=recv_sem.at[k],
            device_id=to,
            device_id_type=MESH,
        )

    def send(k, carry):
        copy(k).start()
        return carry

    lax.fori_loop(1, n, send, 0)

    def take(k, total):
        copy(k).wait_recv()
        return total + held[k]

    total = lax.fori_loop(1, n, take, parts_ref[me])

    def sent(k, carry):
        copy(k).wait_send()
        return carry

    lax.fori_loop(1, n, sent, 0)
    counts = total[:, shells : shells + 1]
    out_ref[...] = total[:, :shells] / (2.0 * counts * weight_ref[...])


def exchange(sizes, parts, weight):
    n = sizes[0] * sizes[1]
    shells = weight.shape[1]
    vmem = pl.BlockSpec(memory_space=pltpu.VMEM)
    return pl.pallas_call(
        functools.partial(exchange_kernel, sizes, shells),
        out_shape=jax.ShapeDtypeStruct((GROUPS_DEV, shells), jnp.float32),
        in_specs=[vmem, vmem],
        out_specs=vmem,
        scratch_shapes=[
            pltpu.VMEM((n, GROUPS_DEV, parts.shape[-1]), jnp.float32),
            pltpu.SemaphoreType.DMA((n,)),
            pltpu.SemaphoreType.DMA((n,)),
        ],
        compiler_params=pltpu.CompilerParams(collective_id=1, has_side_effects=True),
        name="exchange_groups",
    )(parts.reshape(n, GROUPS_DEV, parts.shape[-1]), weight)


def body(sizes, images, slices, classes, rotations, defocus, groups):
    doms, clss = sizes
    n = doms * clss
    count, _, pixels = images.shape
    side = math.isqrt(pixels)
    classes_here, rot_count = slices.shape[:2]

    def rows_of(array):
        lead = array.shape[:-2]
        split = array.reshape(lead + (2, side, side))
        return jnp.swapaxes(split, -3, -2).reshape(lead + (2 * side, side))

    own = rows_of(slices).reshape(classes_here * rot_count, 2 * side, side)
    ny = clss // 2
    if clss % 2 == 0 and doms % ny == 0 and n <= 32:
        every = gather((ny, ny, doms // ny), own)
    else:
        every = lax.all_gather(own, AXES, axis=0)
    every = every.reshape(n * own.shape[0], 2 * side, side)
    index = classes * rot_count + rotations
    parts = shell_power(rows_of(images), every, index, defocus, groups, GROUPS_DEV * n)
    offsets = np.arange(side)
    signed = np.where(offsets < side // 2, offsets, offsets - side)
    radius = signed[:, None] ** 2 + signed[None, :] ** 2
    s = np.arange(side // 2)[:, None, None]
    weight = ((s * s <= radius) & (radius < (s + 1) ** 2)).sum(axis=(1, 2)).astype(np.float32)
    return exchange(sizes, parts, jnp.asarray(weight).reshape(1, -1))


def solution(mesh):
    sizes = (mesh.shape["dom"], mesh.shape["cls"])
    return jax.shard_map(
        functools.partial(body, sizes),
        mesh=mesh,
        in_specs=(
            P(AXES, None, None),
            P(AXES, None, None, None),
            P(AXES),
            P(AXES),
            P(AXES),
            P(AXES),
        ),
        out_specs=P(AXES, None),
        check_vma=False,
    )
```

time: 307 us -> 92.3 us (0.30)
  waiting for transfers between devices: 127 us -> 0 us
  Pallas kernels: 0 us -> 84.7 us
  other arithmetic: 74.4 us -> 1.34 us
  blocking collectives: 42.6 us -> 0 us
  local copies, waits for them, and re-layouts: 41.3 us -> 6.09 us
  between operations: 13.4 us -> 0.05 us
  matrix products: 8.71 us -> 0 us
    unnamed x3 -> x0, waiting for transfers between devices: 123 us -> none
    pallas_call x0 -> x3, Pallas kernels: none -> 84.7 us  [the longest x1 45 us: gather(): pl.pallas_call(functools.partial(gather_kernel, shape), out_shape=jax.Sha...]
    unnamed x1 -> x0, blocking collectives: 42.6 us -> none
    reduce_sum x3 -> x0, other arithmetic: 38.8 us -> none  [the longest x1 37.1 us: power_in_shells(): pixel_power = jnp.sum(difference * difference, axis=1)]
    neg x1 -> x0, other arithmetic: 32 us -> none  [contrast(): -(math.sqrt(1.0 - AMPLITUDE * AMPLITUDE) * jnp.sin(phase_shift) + AMPLITU...]
    gather x1 -> x0, local copies, waits for them, and re-layouts: 23.2 us -> none  [body(): shard_rows.reshape(shard_count * rotation_count, 2, pixel_count)[row_index]]
    all_gather x1 -> x0, local copies, waits for them, and re-layouts: 16.3 us -> none  [body(): shard_rows = lax.all_gather(slices, ('dom', 'cls'), axis=0, tiled=True)]
    dot_general x2 -> x0, matrix products: 8.71 us -> none  [the longest x1 7.72 us: power_in_shells(): jnp.dot(pixel_power, shell_table, precision=lax.Precision.HIGHEST, prefer...]
  transfers between devices with their start and end apart: 2 -> 0, of which waited for: 2 -> 0; matrix products, arithmetic and copies ran while one was open for 12% -> 0% of each run, Pallas kernels for 0% -> 0%
where the time goes in v1:
time: 92.3 us; the launch traced here: 92.1 us
  Pallas kernels  84.7 us (92%)
  local copies, waits for them, and re-layouts  6.09 us (7%)
  other arithmetic  1.34 us (1%)
    pallas_call x1, Pallas kernels, gather(): pl.pallas_call(functools.partial(gather_kernel, shape), out_shape=jax.Sha...  45 us
    pallas_call x1, Pallas kernels, shell_power(): pl.pallas_call(functools.partial(power_kernel, side, 4), grid=(rows // ch...  29.5 us
    pallas_call x1, Pallas kernels, exchange(): pl.pallas_call(functools.partial(exchange_kernel, sizes, shells), out_sha...  10.1 us
    unnamed x13, local copies, waits for them, and re-layouts  6.09 us

profile of v1, /device:TPU:0, one launch (start us, length us, event | category | flops | bytes accessed | tf_op | source)
XLA Modules:
  0.0 92.1 jit_solution(17104987178186366123)
XLA Ops:
  0.0 0.0 copy-start.5
  0.0 0.7 multiply_add_fusion.index_ref
  0.7 0.7 convert_element_type.3.depth_ref
  1.3 0.0 copy-start.2
  1.4 0.9 %copy-done.2 = bf16[1,4,2,16384]{3,2,1,0:T(2,128)(2,1)S(1)} copy-done((bf16[1,4,2,16384]{3,2,1,0:T(2,128)(2,1)S(1)}, bf16[1,4,2,16384]{3,2,1,0:T(2,128)(2,1)}, u32[]{:S(2)}) %copy-start.2) | copy-done | bytes 262168
  2.3 0.0 copy-start.3
  2.3 0.0 copy-start.4
  2.3 45.0 %gather_slices.1 = bf16[32,4,256,128]{3,2,1,0:T(8,128)(2,1)S(1)} custom-call(bf16[4,256,128]{2,1,0:T(8,128)(2,1)S(1)} %bitcast.15), custom_call_target="tpu_custom_call" | custom-call | tf_op jit(solution)/shard_map/gather_slices/pallas_call | solution.py:183
  47.3 0.0 copy-start
  47.3 3.2 %copy-done = bf16[32,4,256,128]{3,2,1,0:T(8,128)(2,1)} copy-done((bf16[32,4,256,128]{3,2,1,0:T(8,128)(2,1)}, bf16[32,4,256,128]{3,2,1,0:T(8,128)(2,1)S(1)}, u32[]{:S(2)}) %copy-start) | copy-done | bytes 8388632
  50.6 0.0 copy-done.5
  50.6 0.0 copy-done.3
  50.6 0.0 copy-done.4
  50.6 29.5 %shell_power.1 = f32[256,128]{1,0:T(8,128)S(1)} custom-call(s32[128]{0:T(128)S(1)} %multiply_add_fusion.index_ref, f32[128]{0:T(128)S(1)} %convert_element_type.3.depth_ref, bf16[128,256,128]{2,1,0:T(8,128)(2,1)} %bitcast.17, bf16[128,256,128]{2,1,0:T(8,128)(2,1)} %bitcast.13, f32[256,128]{1,0:T(8,128)S(1)} %copy-done.4, f32[256,128]{1,0:T(8,128)S(1)} %copy-done.3, ...), custom_call_target="tpu_custom_call" | custom-call | tf_op jit(solution)/shard_map/shell_power/pallas_call | solution.py:270
  80.1 0.0 copy-start.1
  80.1 0.6 copy-done.1
  80.7 10.1 %exchange_groups.1 = f32[8,64]{1,0:T(8,128)} custom-call(f32[32,8,128]{2,1,0:T(8,128)} %bitcast.14, f32[1,64]{1,0:T(1,128)} %constant.12.weight_ref), custom_call_target="tpu_custom_call" | custom-call | tf_op jit(solution)/shard_map/exchange_groups/pallas_call | solution.py:346
  90.9 1.3 %copy.13 = f32[8,64]{1,0:T(8,128)} copy(f32[8,64]{1,0:T(8,128)} %exchange_groups.1) | data formatting | bytes 4096
Async XLA Ops:
  0.0 50.6 %copy-start.5 = (s32[128]{0:T(128)S(1)}, s32[128]{0:T(128)}, u32[]{:S(2)}) copy-start(s32[128]{0:T(128)} %param.14) | copy-start | bytes 1540
  1.3 0.9 %copy-start.2 = (bf16[1,4,2,16384]{3,2,1,0:T(2,128)(2,1)S(1)}, bf16[1,4,2,16384]{3,2,1,0:T(2,128)(2,1)}, u32[]{:S(2)}) copy-start(bf16[1,4,2,16384]{3,2,1,0:T(2,128)(2,1)} %param.10) | copy-start | bytes 786436
  2.3 48.3 %copy-start.3 = (f32[256,128]{1,0:T(8,128)S(1)}, f32[256,128]{1,0:T(8,128)}, u32[]{:S(2)}) copy-start(f32[256,128]{1,0:T(8,128)} %constant.9.clone.offset_ref) | copy-start | bytes 393220
  2.3 48.3 %copy-start.4 = (f32[256,128]{1,0:T(8,128)S(1)}, f32[256,128]{1,0:T(8,128)}, u32[]{:S(2)}) copy-start(f32[256,128]{1,0:T(8,128)} %constant.8.clone.slope_ref) | copy-start | bytes 393220
  47.3 3.2 %copy-start = (bf16[32,4,256,128]{3,2,1,0:T(8,128)(2,1)}, bf16[32,4,256,128]{3,2,1,0:T(8,128)(2,1)S(1)}, u32[]{:S(2)}) copy-start(bf16[32,4,256,128]{3,2,1,0:T(8,128)(2,1)S(1)} %gather_slices.1) | copy-start | bytes 25165828
  80.1 0.6 copy-start.1

commit v2 on v1

--- a/solution.py
+++ b/solution.py
@@ -14,6 +14,7 @@
 WAVELENGTH = 0.0197
 SPHERICAL = 27000000.0
 AMPLITUDE = 0.1
+ROUND = 12582912.0
 MESH = pl.DeviceIdType.MESH
 AXES = ("dom", "cls")
 ROUTES = (("x", "y", "z"), ("z", "y", "x"), ("z", "x", "y"))
@@ -193,18 +194,19 @@
             pltpu.SemaphoreType.DMA((3, devices)),
         ],
         compiler_params=pltpu.CompilerParams(
-            collective_id=0, has_side_effects=True, vmem_limit_bytes=32 * 1024 * 1024
+            collective_id=0, has_side_effects=True, vmem_limit_bytes=12 * 1024 * 1024
         ),
         name="gather_slices",
     )(own)
 
 
 def power_kernel(
-    side, rot_count, index_ref, depth_ref, images_ref, slices_ref, slope_ref, offset_ref, groups_ref, out_ref, power, acc
+    side, rot_count, classes_ref, rotations_ref, defocus_ref, images_ref, slices_ref, slope_ref, offset_ref, groups_ref, out_ref, power, acc
 ):
     step = pl.program_id(0)
     count, chunk, lanes = images_ref.shape
     shells = side // 2
+    pitch = power.shape[0] // count
 
     @pl.when(step == 0)
     def _():
@@ -214,15 +216,15 @@
     offset = offset_ref[...]
 
     def one(i, carry):
-        turns = depth_ref[i] * slope + offset
-        x = turns - jnp.round(turns)
+        turns = defocus_ref[i].astype(jnp.float32) * slope + offset
+        x = turns - ((turns + ROUND) - ROUND)
         y = x * x
         s = jnp.full_like(y, SINE[-1])
         for value in SINE[-2::-1]:
             s = s * y + value
         s = s * x
-        d = images_ref[i].astype(jnp.float32) + s * slices_ref[index_ref[i], pl.ds(pl.multiple_of(step * chunk, chunk), chunk), :].astype(jnp.float32)
-        power[pl.ds(pl.multiple_of(i * chunk, chunk), chunk), :] = d * d
+        d = images_ref[i].astype(jnp.float32) + s * slices_ref[classes_ref[i] * rot_count + rotations_ref[i]].astype(jnp.float32)
+        power[pl.ds(pl.multiple_of(i * pitch, 8), chunk), :] = d * d
         return carry
 
     lax.fori_loop(0, count, one, 0, unroll=4)
@@ -236,12 +238,13 @@
         fa = jnp.where(a < side // 2, a, a - side)
         r = fa * fa + fb * fb
         table = jnp.where((s * s <= r) & (r < (s + 1) * (s + 1)), 1.0, 0.0).astype(jnp.bfloat16)
-        p = power[pl.ds(2 * k, count, stride=chunk), :] + power[pl.ds(2 * k + 1, count, stride=chunk), :]
+        p = power[pl.ds(2 * k, count, stride=pitch), :] + power[pl.ds(2 * k + 1, count, stride=pitch), :]
         high = p.astype(jnp.bfloat16)
         low = (p - high.astype(jnp.float32)).astype(jnp.bfloat16)
-        total = total + (
-            jnp.dot(high, table, preferred_element_type=jnp.float32)
-            + jnp.dot(low, table, preferred_element_type=jnp.float32)
+        total = total + jnp.dot(
+            jnp.concatenate([high, low], axis=1),
+            jnp.concatenate([table, table], axis=0),
+            preferred_element_type=jnp.float32,
         )
     acc[...] = total
 
@@ -256,7 +259,7 @@
         )
 
 
-def shell_power(images, slices, index, defocus, groups, group_total):
+def shell_power(images, slices, classes, rotations, rot_count, defocus, groups, group_total):
     count, rows, side = images.shape
     chunk = 32
     offsets = np.arange(side)
@@ -268,26 +271,27 @@
     offset = (offset - np.round(offset)).astype(np.float32)
     smem = pl.BlockSpec(memory_space=pltpu.SMEM)
     return pl.pallas_call(
-        functools.partial(power_kernel, side, 4),
+        functools.partial(power_kernel, side, rot_count),
         grid=(rows // chunk,),
         out_shape=jax.ShapeDtypeStruct((group_total, 128), jnp.float32),
         in_specs=[
             smem,
             smem,
+            smem,
             pl.BlockSpec((count, chunk, side), lambda i: (0, i, 0)),
-            pl.BlockSpec(memory_space=pltpu.VMEM),
+            pl.BlockSpec((slices.shape[0], chunk, side), lambda i: (0, i, 0)),
             pl.BlockSpec((chunk, side), lambda i: (i, 0)),
             pl.BlockSpec((chunk, side), lambda i: (i, 0)),
             pl.BlockSpec((1, count), lambda i: (0, 0)),
         ],
         out_specs=pl.BlockSpec((group_total, 128), lambda i: (0, 0)),
         scratch_shapes=[
-            pltpu.VMEM((count * chunk, side), jnp.float32),
+            pltpu.VMEM((count * (chunk + 8), side), jnp.float32),
             pltpu.VMEM((count, side // 2), jnp.float32),
         ],
-        compiler_params=pltpu.CompilerParams(vmem_limit_bytes=48 * 1024 * 1024),
+        compiler_params=pltpu.CompilerParams(vmem_limit_bytes=20 * 1024 * 1024),
         name="shell_power",
-    )(index, defocus.astype(jnp.float32), images, slices, jnp.asarray(slope), jnp.asarray(offset), groups.reshape(1, count))
+    )(classes, rotations, defocus, images, slices, jnp.asarray(slope), jnp.asarray(offset), groups.reshape(1, count))
 
 
 def exchange_kernel(sizes, shells, parts_ref, weight_ref, out_ref, held, send_sem, recv_sem):
@@ -353,7 +357,9 @@
             pltpu.SemaphoreType.DMA((n,)),
             pltpu.SemaphoreType.DMA((n,)),
         ],
-        compiler_params=pltpu.CompilerParams(collective_id=1, has_side_effects=True),
+        compiler_params=pltpu.CompilerParams(
+            collective_id=1, has_side_effects=True, vmem_limit_bytes=4 * 1024 * 1024
+        ),
         name="exchange_groups",
     )(parts.reshape(n, GROUPS_DEV, parts.shape[-1]), weight)
 
@@ -377,8 +383,7 @@
     else:
         every = lax.all_gather(own, AXES, axis=0)
     every = every.reshape(n * own.shape[0], 2 * side, side)
-    index = classes * rot_count + rotations
-    parts = shell_power(rows_of(images), every, index, defocus, groups, GROUPS_DEV * n)
+    parts = shell_power(rows_of(images), every, classes, rotations, rot_count, defocus, groups, GROUPS_DEV * n)
     offsets = np.arange(side)
     signed = np.where(offsets < side // 2, offsets, offsets - side)
     radius = signed[:, None] ** 2 + signed[None, :] ** 2

time: 92.3 us -> 78.4 us (0.85)
  Pallas kernels: 84.7 us -> 76.4 us
  local copies, waits for them, and re-layouts: 6.09 us -> 1.73 us
  other arithmetic: 1.34 us -> 0 us
    pallas_call x1, Pallas kernels: 29.5 us -> 22.4 us  [shell_power(): pl.pallas_call(functools.partial(power_kernel, side, rot_count), grid=(ro...]
    unnamed x13 -> x19, local copies, waits for them, and re-layouts: 6.09 us -> 1.73 us
    pallas_call x1, Pallas kernels: 10.1 us -> 8.93 us  [exchange(): pl.pallas_call(functools.partial(exchange_kernel, sizes, shells), out_sha...]
where the time goes in v2:
time: 78.4 us; the launch traced here: 78.3 us
  Pallas kernels  76.4 us (97%)
  local copies, waits for them, and re-layouts  1.73 us (2%)
    pallas_call x1, Pallas kernels, gather(): pl.pallas_call(functools.partial(gather_kernel, shape), out_shape=jax.Sha...  45.1 us
    pallas_call x1, Pallas kernels, shell_power(): pl.pallas_call(functools.partial(power_kernel, side, rot_count), grid=(ro...  22.4 us
    pallas_call x1, Pallas kernels, exchange(): pl.pallas_call(functools.partial(exchange_kernel, sizes, shells), out_sha...  8.93 us
    unnamed x19, local copies, waits for them, and re-layouts  1.73 us

profile of v2, /device:TPU:0, one launch (start us, length us, event | category | flops | bytes accessed | tf_op | source)
XLA Modules:
  0.0 78.3 jit_solution(4591015053978210925)
XLA Ops:
  0.0 0.0 copy-start
  0.0 0.0 copy-start.1
  0.0 1.1 %copy-done.1 = bf16[1,4,2,16384]{3,2,1,0:T(2,128)(2,1)S(1)} copy-done((bf16[1,4,2,16384]{3,2,1,0:T(2,128)(2,1)S(1)}, bf16[1,4,2,16384]{3,2,1,0:T(2,128)(2,1)}, u32[]{:S(2)}) %copy-start.1) | copy-done | bytes 262168
  1.1 0.0 copy-start.2
  1.1 0.0 copy-start.3
  1.1 0.0 copy-start.4
  1.1 0.0 copy-start.5
  1.1 0.0 copy-start.6
  1.1 0.0 copy-start.7
  1.1 45.1 %gather_slices.1 = bf16[32,4,256,128]{3,2,1,0:T(8,128)(2,1)S(1)} custom-call(bf16[4,256,128]{2,1,0:T(8,128)(2,1)S(1)} %bitcast.16), custom_call_target="tpu_custom_call" | custom-call | tf_op jit(solution)/shard_map/gather_slices/pallas_call | solution.py:184
  46.2 0.0 copy-done
  46.2 0.0 copy-done.2
  46.2 0.0 copy-done.3
  46.2 0.0 copy-done.4
  46.2 0.0 copy-done.5
  46.3 0.0 copy-done.6
  46.3 0.0 copy-done.7
  46.3 0.0 copy-start.8
  46.3 22.4 %shell_power.1 = f32[256,128]{1,0:T(8,128)S(1)} custom-call(s32[128]{0:T(128)S(1)} %copy-done.4, s32[128]{0:T(128)S(1)} %copy-done.5, s32[128]{0:T(128)S(1)} %copy-done.6, bf16[128,256,128]{2,1,0:T(8,128)(2,1)S(1)} %bitcast.14, bf16[128,256,128]{2,1,0:T(8,128)(2,1)S(1)} %bitcast.13, f32[256,128]{1,0:T(8,128)S(1)} %copy-done.3, f32[256,128]{1,0:T(8,128)S(1)} %copy-done.2, ...), custom_call_target="tpu_custom_call" | custom-call | tf_op jit(solution)/shard_map/shell_power/pallas_call | solution.py:273
  68.7 0.0 copy-done.8
  68.7 8.9 %exchange_groups.1 = f32[8,64]{1,0:T(8,128)S(1)} custom-call(f32[32,8,128]{2,1,0:T(8,128)S(1)} %bitcast.15, f32[1,64]{1,0:T(1,128)S(1)} %copy-done.8), custom_call_target="tpu_custom_call" | custom-call | tf_op jit(solution)/shard_map/exchange_groups/pallas_call | solution.py:350
  77.7 0.6 copy.13
Async XLA Ops:
  0.0 46.2 %copy-start = (bf16[128,2,16384]{2,1,0:T(2,128)(2,1)S(1)}, bf16[128,2,16384]{2,1,0:T(2,128)(2,1)}, u32[]{:S(2)}) copy-start(bf16[128,2,16384]{2,1,0:T(2,128)(2,1)} %param.9) | copy-start | bytes 25165828
  0.0 1.1 %copy-start.1 = (bf16[1,4,2,16384]{3,2,1,0:T(2,128)(2,1)S(1)}, bf16[1,4,2,16384]{3,2,1,0:T(2,128)(2,1)}, u32[]{:S(2)}) copy-start(bf16[1,4,2,16384]{3,2,1,0:T(2,128)(2,1)} %param.10) | copy-start | bytes 786436
  1.1 45.1 %copy-start.2 = (f32[256,128]{1,0:T(8,128)S(1)}, f32[256,128]{1,0:T(8,128)}, u32[]{:S(2)}) copy-start(f32[256,128]{1,0:T(8,128)} %constant.7.clone.offset_ref) | copy-start | bytes 393220
  1.1 45.1 %copy-start.3 = (f32[256,128]{1,0:T(8,128)S(1)}, f32[256,128]{1,0:T(8,128)}, u32[]{:S(2)}) copy-start(f32[256,128]{1,0:T(8,128)} %constant.6.clone.slope_ref) | copy-start | bytes 393220
  1.1 45.1 %copy-start.4 = (s32[128]{0:T(128)S(1)}, s32[128]{0:T(128)}, u32[]{:S(2)}) copy-start(s32[128]{0:T(128)} %classes_ref.1) | copy-start | bytes 1540
  1.1 45.1 %copy-start.5 = (s32[128]{0:T(128)S(1)}, s32[128]{0:T(128)}, u32[]{:S(2)}) copy-start(s32[128]{0:T(128)} %rotations_ref.1) | copy-start | bytes 1540
  1.1 45.1 %copy-start.6 = (s32[128]{0:T(128)S(1)}, s32[128]{0:T(128)}, u32[]{:S(2)}) copy-start(s32[128]{0:T(128)} %defocus_ref.1) | copy-start | bytes 1540
  1.1 45.1 %copy-start.7 = (s32[128]{0:T(128)S(1)}, s32[128]{0:T(128)}, u32[]{:S(2)}) copy-start(s32[128]{0:T(128)} %param.14) | copy-start | bytes 1540
  46.3 22.5 %copy-start.8 = (f32[1,64]{1,0:T(1,128)S(1)}, f32[1,64]{1,0:T(1,128)}, u32[]{:S(2)}) copy-start(f32[1,64]{1,0:T(1,128)} %constant.10.weight_ref) | copy-start | bytes 772

commit v3 on v2

--- a/solution.py
+++ b/solution.py
@@ -28,7 +28,7 @@
     return np.linalg.lstsq(basis, np.sin(2 * math.pi * nodes), rcond=None)[0]
 
 
-SINE = [float(v) for v in sine_coefficients(6)]
+SINE = [float(v) for v in sine_coefficients(5)]
 
 
 def gather_kernel(shape, own_ref, out_ref, local_sem, send_sem, recv_sem, pair_send, pair_recv):
@@ -227,7 +227,7 @@
         power[pl.ds(pl.multiple_of(i * pitch, 8), chunk), :] = d * d
         return carry
 
-    lax.fori_loop(0, count, one, 0, unroll=4)
+    lax.fori_loop(0, count, one, 0, unroll=8)
 
     b = lax.broadcasted_iota(jnp.int32, (lanes, shells), 0)
     s = lax.broadcasted_iota(jnp.int32, (lanes, shells), 1)

time: 78.4 us -> 75.6 us (0.964)
  Pallas kernels: 76.4 us -> 73.6 us
    pallas_call x1, Pallas kernels: 22.4 us -> 19.6 us  [shell_power(): pl.pallas_call(functools.partial(power_kernel, side, rot_count), grid=(ro...]
where the time goes in v3:
time: 75.6 us; the launch traced here: 75.5 us
  Pallas kernels  73.6 us (97%)
  local copies, waits for them, and re-layouts  1.73 us (2%)
    pallas_call x1, Pallas kernels, gather(): pl.pallas_call(functools.partial(gather_kernel, shape), out_shape=jax.Sha...  45.1 us
    pallas_call x1, Pallas kernels, shell_power(): pl.pallas_call(functools.partial(power_kernel, side, rot_count), grid=(ro...  19.6 us
    pallas_call x1, Pallas kernels, exchange(): pl.pallas_call(functools.partial(exchange_kernel, sizes, shells), out_sha...  8.93 us
    unnamed x19, local copies, waits for them, and re-layouts  1.73 us

profile of v3, /device:TPU:0, one launch (start us, length us, event | category | flops | bytes accessed | tf_op | source)
XLA Modules:
  0.0 75.5 jit_solution(4752210385902485538)
XLA Ops:
  0.0 0.0 copy-start
  0.0 0.0 copy-start.1
  0.0 1.1 %copy-done.1 = bf16[1,4,2,16384]{3,2,1,0:T(2,128)(2,1)S(1)} copy-done((bf16[1,4,2,16384]{3,2,1,0:T(2,128)(2,1)S(1)}, bf16[1,4,2,16384]{3,2,1,0:T(2,128)(2,1)}, u32[]{:S(2)}) %copy-start.1) | copy-done | bytes 262168
  1.1 0.0 copy-start.2
  1.1 0.0 copy-start.3
  1.1 0.0 copy-start.4
  1.1 0.0 copy-start.5
  1.1 0.0 copy-start.6
  1.1 0.0 copy-start.7
  1.1 45.1 %gather_slices.1 = bf16[32,4,256,128]{3,2,1,0:T(8,128)(2,1)S(1)} custom-call(bf16[4,256,128]{2,1,0:T(8,128)(2,1)S(1)} %bitcast.16), custom_call_target="tpu_custom_call" | custom-call | tf_op jit(solution)/shard_map/gather_slices/pallas_call | solution.py:184
  46.2 0.0 copy-done
  46.2 0.0 copy-done.2
  46.2 0.0 copy-done.3
  46.2 0.0 copy-done.4
  46.2 0.0 copy-done.5
  46.3 0.0 copy-done.6
  46.3 0.0 copy-done.7
  46.3 0.0 copy-start.8
  46.3 19.6 %shell_power.1 = f32[256,128]{1,0:T(8,128)S(1)} custom-call(s32[128]{0:T(128)S(1)} %copy-done.4, s32[128]{0:T(128)S(1)} %copy-done.5, s32[128]{0:T(128)S(1)} %copy-done.6, bf16[128,256,128]{2,1,0:T(8,128)(2,1)S(1)} %bitcast.14, bf16[128,256,128]{2,1,0:T(8,128)(2,1)S(1)} %bitcast.13, f32[256,128]{1,0:T(8,128)S(1)} %copy-done.3, f32[256,128]{1,0:T(8,128)S(1)} %copy-done.2, ...), custom_call_target="tpu_custom_call" | custom-call | tf_op jit(solution)/shard_map/shell_power/pallas_call | solution.py:273
  65.9 0.0 copy-done.8
  65.9 8.9 %exchange_groups.1 = f32[8,64]{1,0:T(8,128)S(1)} custom-call(f32[32,8,128]{2,1,0:T(8,128)S(1)} %bitcast.15, f32[1,64]{1,0:T(1,128)S(1)} %copy-done.8), custom_call_target="tpu_custom_call" | custom-call | tf_op jit(solution)/shard_map/exchange_groups/pallas_call | solution.py:350
  74.9 0.6 copy.13
Async XLA Ops:
  0.0 46.2 %copy-start = (bf16[128,2,16384]{2,1,0:T(2,128)(2,1)S(1)}, bf16[128,2,16384]{2,1,0:T(2,128)(2,1)}, u32[]{:S(2)}) copy-start(bf16[128,2,16384]{2,1,0:T(2,128)(2,1)} %param.9) | copy-start | bytes 25165828
  0.0 1.1 %copy-start.1 = (bf16[1,4,2,16384]{3,2,1,0:T(2,128)(2,1)S(1)}, bf16[1,4,2,16384]{3,2,1,0:T(2,128)(2,1)}, u32[]{:S(2)}) copy-start(bf16[1,4,2,16384]{3,2,1,0:T(2,128)(2,1)} %param.10) | copy-start | bytes 786436
  1.1 45.1 %copy-start.2 = (f32[256,128]{1,0:T(8,128)S(1)}, f32[256,128]{1,0:T(8,128)}, u32[]{:S(2)}) copy-start(f32[256,128]{1,0:T(8,128)} %constant.7.clone.offset_ref) | copy-start | bytes 393220
  1.1 45.1 %copy-start.3 = (f32[256,128]{1,0:T(8,128)S(1)}, f32[256,128]{1,0:T(8,128)}, u32[]{:S(2)}) copy-start(f32[256,128]{1,0:T(8,128)} %constant.6.clone.slope_ref) | copy-start | bytes 393220
  1.1 45.1 %copy-start.4 = (s32[128]{0:T(128)S(1)}, s32[128]{0:T(128)}, u32[]{:S(2)}) copy-start(s32[128]{0:T(128)} %classes_ref.1) | copy-start | bytes 1540
  1.1 45.1 %copy-start.5 = (s32[128]{0:T(128)S(1)}, s32[128]{0:T(128)}, u32[]{:S(2)}) copy-start(s32[128]{0:T(128)} %rotations_ref.1) | copy-start | bytes 1540
  1.1 45.1 %copy-start.6 = (s32[128]{0:T(128)S(1)}, s32[128]{0:T(128)}, u32[]{:S(2)}) copy-start(s32[128]{0:T(128)} %defocus_ref.1) | copy-start | bytes 1540
  1.1 45.1 %copy-start.7 = (s32[128]{0:T(128)S(1)}, s32[128]{0:T(128)}, u32[]{:S(2)}) copy-start(s32[128]{0:T(128)} %param.14) | copy-start | bytes 1540
  46.3 19.6 %copy-start.8 = (f32[1,64]{1,0:T(1,128)S(1)}, f32[1,64]{1,0:T(1,128)}, u32[]{:S(2)}) copy-start(f32[1,64]{1,0:T(1,128)} %constant.10.weight_ref) | copy-start | bytes 772
